TPU v7x, 256 devices: a whole 4x4x8 slice. The times are simulated.
256 devices in a mesh: unit: 4 (over y), bank: 4 (over x), zero: 16 (over z, core).
Axes of the slice: x: 4, y: 4, z: 8, core: 2. Of those that a mesh axis runs over, the one named last changes fastest.
Arguments:
- train_down: float32 [256, 1024, 2048], P(('unit', 'bank'), None, 'zero'), parts along dimension 0, may hold values from -0.25 to 0.25
- router_weight: float32 [8192, 64], P(('unit', 'zero'), 'bank'), parts along dimension 0, may hold values from -0.125 to 0.125
- router_gain: float32 [8192], P(('unit', 'zero')), parts along dimension 0, may hold values from 0.25 to 1.75
Outputs:
- ready_down: bfloat16 [256, 1024, 2048], P(('unit', 'bank'), 'zero'), parts along dimension 0
- scale_down: float32 [256, 1024], P(('unit', 'bank'), 'zero'), parts along dimension 0
- serve_router: bfloat16 [8192, 64], P('unit'), parts along dimension 0
There are 4 independent parts, one for each index of `unit`. A program takes and returns all parts, laid end to end along the dimension named above; each array names one. Nothing has to cross between parts.
All inputs are finite; a program needn't handle non-finite values.
Results may differ from a plain program's by a relative error of at most 0.001.
Values may be sent and summed in bfloat16 or wider, within the bound.
A program may use at most 128 MiB of HBM per device.

v0:
```python
import jax
import jax.numpy as jnp
from jax import lax
from jax.sharding import Mesh
from jax.sharding import PartitionSpec as P

ZERO = ("zero_0", "zero_1")
UNIT_ZERO = ("unit", "zero_0", "zero_1")


def gathered_total(value, axis):
    tiles = lax.all_gather(value, axis)
    return tiles.max(axis=0)


def in_blocks(value, dim, length):
    return jnp.stack(jnp.split(value, length, axis=dim))


def joined_along(tiles, dim):
    tiles = jnp.moveaxis(tiles, 0, dim)
    dims = tiles.shape
    return tiles.reshape(*dims[:dim], dims[dim] * dims[dim + 1], *dims[dim + 2 :])


def turned_blocks(tiles, axes, sequence):
    dims = [lax.axis_size(a) for a in axes]
    tiles = tiles.reshape(*dims, *tiles.shape[1:])
    for k in sequence:
        tiles = lax.all_to_all(tiles, axes[k], split_axis=k, concat_axis=k, tiled=True)
    return tiles.reshape(-1, *tiles.shape[len(axes) :])


def two_step_exchange(value, groups, sequence, split_dim, concat_dim):
    length = lax.axis_size(groups[0]) * lax.axis_size(groups[1])
    tiles = in_blocks(value, split_dim, length)
    return joined_along(turned_blocks(tiles, groups, sequence), concat_dim)


def per_device(train_down, router_weight, router_gain):
    scale_down = gathered_total(jnp.max(jnp.abs(train_down), axis=2), ZERO)
    narrow_down = (train_down / jnp.expand_dims(scale_down, 2)).astype(jnp.bfloat16)
    ready_down = two_step_exchange(narrow_down, ("zero_0", "zero_1"), (1, 0), 1, 2)
    scale_down = lax.dynamic_slice_in_dim(
        scale_down, lax.axis_index(ZERO) * ready_down.shape[1], ready_down.shape[1], axis=1
    )
    part_router = (router_weight * router_gain[:, None]).astype(jnp.bfloat16)
    row_router = lax.all_gather(part_router, ZERO, axis=0, tiled=True)
    serve_router = lax.all_gather(row_router, "bank", axis=1, tiled=True)
    return (ready_down, scale_down, serve_router)


def solution(mesh):
    torus = Mesh(
        mesh.devices.reshape(mesh.shape["unit"], mesh.shape["bank"], 8, 2),
        ("unit", "bank", "zero_0", "zero_1"),
    )
    placed = (P(("unit", "bank"), None, ZERO), P(UNIT_ZERO, "bank"), P(UNIT_ZERO))
    return jax.shard_map(
        per_device,
        mesh=torus,
        in_specs=placed,
        out_specs=(P(("unit", "bank"), ZERO, None), P(("unit", "bank"), ZERO), P("unit", None)),
        check_vma=False,
    )
```

profile of v0, /device:TPU:1, one launch (start us, length us, event | category | flops | bytes accessed | tf_op | source)
XLA Modules:
  0.0 207.9 jit_solution(14406718394577058157)
XLA Ops:
  7.2 0.0 all-gather.3.cloned.1.call-start
  7.2 6.2 %abs_reduce_fusion = f32[16,1024]{1,0:T(8,128)} fusion(f32[16,1024,128]{2,1,0:T(8,128)} %param.3), kind=kLoop, calls=%fused_computation.1 | loop fusion | flops 4177920 | bytes 8454144 | tf_op jit(solution)/shard_map/reduce_max | solution.py:41
  13.5 0.0 all-gather.3.cloned.1.call-update
  13.5 42.8 %all-gather.3.cloned.1.call-done = f32[256,1024]{1,0:T(8,128)} async-done(((f32[16,1024]{1,0:T(8,128)}), f32[256,1024]{1,0:T(8,128)}) %all-gather.3.cloned.1.call-update) | async-done | bytes 1048592 | tf_op jit(solution)/shard_map/all_gather | solution.py:12
  56.3 1.3 reduce_max.19
  57.6 5.3 %divide_convert_fusion = bf16[16,1024,128]{2,1,0:T(8,128)(2,1)S(1)} fusion(f32[16,1024,128]{2,1,0:T(8,128)} %param.3, f32[16,1024]{1,0:T(8,128)S(1)} %reduce_max.19), kind=kLoop, calls=%fused_computation | loop fusion | flops 4194304 | bytes 12648448 | tf_op jit(solution)/shard_map/convert_element_type | solution.py:42
  63.5 1.3 copy.12
  64.8 7.1 %all_to_all.10 = bf16[8,2,16,64,128]{4,3,2,0,1:T(8,128)(2,1)S(1)} all-to-all(bf16[8,2,16,64,128]{4,3,2,0,1:T(8,128)(2,1)S(1)} %copy.12), channel_id=1, replica_groups=mesh['unit'=4,'bank'=4,'zero_0'=8,'zero_1'=2] {'zero_1'}, dimensions={1} | all-to-all | bytes 8388608 | tf_op jit(solution)/shard_map/all_to_all | solution.py:30
  71.9 3.0 %copy.13 = bf16[8,2,16,64,128]{4,3,2,1,0:T(8,128)(2,1)} copy(bf16[8,2,16,64,128]{4,3,2,0,1:T(8,128)(2,1)S(1)} %all_to_all.10) | data formatting | bytes 8388608 | tf_op jit(solution)/shard_map/all_to_all | solution.py:30
  74.9 0.0 copy-start
  74.9 0.0 copy-start.1
  74.9 4.7 %all-to-all-start.1 = ((bf16[8,2,16,64,128]{4,3,2,1,0:T(8,128)(2,1)}), bf16[8,2,16,64,128]{4,3,2,1,0:T(8,128)(2,1)}, u32[]{:S(2)}, u32[]{:S(2)}) async-start(bf16[8,2,16,64,128]{4,3,2,1,0:T(8,128)(2,1)} %copy.13), calls=%async_computation.1 | async-start | bytes 8388608 | tf_op jit(solution)/shard_map/all_to_all | solution.py:30
  79.5 0.0 copy-done
  79.6 0.0 copy-done.1
  79.6 104.7 %all_gather.14 = bf16[2048,16]{0,1:T(8,128)(2,1)S(1)} all-gather(bf16[128,16]{0,1:T(8,128)(2,1)S(1)} %multiply_convert_fusion), channel_id=1, replica_groups=mesh['unit'=4,'bank'=4,'zero_0'=8,'zero_1'=2] {'zero_0','zero_1'}, dimensions={0}, use_global_device_ids=true | all-gather | bytes 69632 | tf_op jit(solution)/shard_map/all_gather | solution.py:48
  184.3 10.1 %all_gather.15 = bf16[2048,64]{0,1:T(8,128)(2,1)S(1)} all-gather(bf16[2048,16]{0,1:T(8,128)(2,1)S(1)} %all_gather.14), channel_id=1, replica_groups=mesh['unit'=4,'bank'=4,'zero_0'=8,'zero_1'=2] {'bank'}, dimensions={1}, use_global_device_ids=true | all-gather | bytes 327680 | tf_op jit(solution)/shard_map/all_gather | solution.py:49
  194.3 0.7 constant_dynamic-slice_fusion
  195.0 0.0 all-to-all-done.1
  195.0 5.3 %copy.17 = bf16[16,16,8,8,128]{4,3,0,2,1:T(8,128)(2,1)} copy(bf16[16,16,8,8,128]{4,3,2,1,0:T(8,128)(2,1)} %bitcast.21) | data formatting | bytes 8388608 | tf_op jit(solution)/shard_map/reshape | solution.py:23
  200.4 0.7 copy.34
  (17 shorter events, 0.6 us)
Async XLA Ops:
  7.2 49.1 %all-gather.3.cloned.1.call-start = ((), (), s32[]{:S(2)}) async-start(), calls=%async_computation.2 | async-start | bytes 1114112 | tf_op jit(solution)/shard_map/all_gather | solution.py:12
  74.9 4.7 %copy-start = (f32[128,16]{0,1:T(8,128)S(1)}, f32[128,16]{0,1:T(8,128)}, u32[]{:S(2)}) copy-start(f32[128,16]{0,1:T(8,128)} %param.4) | copy-start | bytes 24580
  74.9 4.7 %copy-start.1 = (f32[128]{0:T(128)S(1)}, f32[128]{0:T(128)}, u32[]{:S(2)}) copy-start(f32[128]{0:T(128)} %param.5) | copy-start | bytes 1540
  74.9 120.2 %all-to-all-start.1 = ((bf16[8,2,16,64,128]{4,3,2,1,0:T(8,128)(2,1)}), bf16[8,2,16,64,128]{4,3,2,1,0:T(8,128)(2,1)}, u32[]{:S(2)}, u32[]{:S(2)}) async-start(bf16[8,2,16,64,128]{4,3,2,1,0:T(8,128)(2,1)} %copy.13), calls=%async_computation.1 | async-start | bytes 8388608 | tf_op jit(solution)/shard_map/all_to_all | solution.py:30
Sparse Core Ops, SparseCore 0:
  13.6 42.6 all-gather.2
where the time goes:
time: 209 us; the launch traced here: 208 us
  blocking collectives  122 us (58%)
  waiting for transfers between devices  42.8 us (20%)
  between operations  14.2 us (7%)
  other arithmetic  12.8 us (6%)
  local copies, waits for them, and re-layouts  11.6 us (6%)
  starting transfers between devices  4.71 us (2%)
    all_gather x1, blocking collectives, per_device(): row_router = lax.all_gather(part_router, ZERO, axis=0, tiled=True)  105 us
    all_gather x1, waiting for transfers between devices, gathered_total(): tiles = lax.all_gather(value, axis)  42.8 us
    all_gather x1, blocking collectives, per_device(): serve_router = lax.all_gather(row_router, 'bank', axis=1, tiled=True)  10.1 us
    all_to_all x1, blocking collectives, turned_blocks(): lax.all_to_all(tiles, axes[k], split_axis=k, concat_axis=k, tiled=True)  7.05 us
    reduce_max x1, other arithmetic, per_device(): scale_down = gathered_total(jnp.max(jnp.abs(train_down), axis=2), ZERO)  6.25 us
    reshape x1, local copies, waits for them, and re-layouts, joined_along(): tiles.reshape(*dims[:dim], dims[dim] * dims[dim + 1], *dims[dim + 2:])  5.35 us
    convert_element_type x1, other arithmetic, per_device(): (train_down / jnp.expand_dims(scale_down, 2)).astype(jnp.bfloat16)  5.26 us
    all_to_all x1, starting transfers between devices, turned_blocks(): lax.all_to_all(tiles, axes[k], split_axis=k, concat_axis=k, tiled=True)  4.67 us
  transfers between devices with their start and end apart: 2, of which 1 were waited for; matrix products, arithmetic and copies ran while one was open for 0% of the time, Pallas kernels for 0%

commit v1 on v0

v1 whole, which is shorter than its diff:
```python
import functools

import jax
import jax.numpy as jnp
from jax import lax
from jax.experimental import pallas as pl
from jax.experimental.pallas import tpu as pltpu
from jax.sharding import PartitionSpec as P

MESH = pl.DeviceIdType.MESH
LANES = 128
EARLY = 2
GROUP = 2

PEERS = [(d, c) for d in (4, 3, 5, 2, 6, 1, 7) for c in (0, 1)] + [(0, 1)]


def exchange_kernel(
    units,
    x_ref, w_ref, g_ref,
    ready_ref, scale_ref, router_ref,
    xv, sent, early, early_in, early_scale, peaks, peaks_in, scales,
    x_sem, send_sem, recv_sem, small_send, small_recv, cross_send, cross_recv,
):
    chips, banks = units
    experts, rows, _ = x_ref.shape
    per = ready_ref.shape[1]
    me = lax.axis_index("zero")
    chip, core = me // 2, lax.rem(me, 2)
    bank = lax.axis_index("bank")
    mine = pl.ds(pl.multiple_of(me * LANES, LANES), LANES)

    def peer(k):
        ahead, other = PEERS[k]
        chip_to = lax.rem(chip + ahead, chips)
        core_to = lax.rem(core + other, 2)
        return chip_to, core_to, chip_to * 2 + core_to

    def load(e):
        return pltpu.make_async_copy(x_ref.at[e], xv.at[e], x_sem.at[e])

    for e in range(experts):
        load(e).start()

    barrier = pltpu.get_barrier_semaphore()
    for k in range(len(PEERS)):
        pl.semaphore_signal(barrier, inc=1, device_id={"zero": peer(k)[2]}, device_id_type=MESH)
    for b in range(1, banks):
        to = lax.rem(bank + b, banks)
        pl.semaphore_signal(barrier, inc=1, device_id={"bank": to}, device_id_type=MESH)

    rank = pl.ds(pl.multiple_of(bank * 16, 16), 16)
    router_ref[rank, mine] = (w_ref[...] * g_ref[...]).astype(jnp.bfloat16)

    def peak(e, block):
        tile = jnp.abs(xv[e, pl.ds(block * LANES, LANES), :])
        return jnp.max(tile.T, axis=0, keepdims=True)

    for e in range(EARLY):
        load(e).wait()
        early[e] = jnp.concatenate([peak(e, b) for b in range(chips)], axis=0)

    pl.semaphore_wait(barrier, len(PEERS) + banks - 1)

    def copy(src, dst, kind, k, to):
        return pltpu.make_async_remote_copy(
            src_ref=src, dst_ref=dst,
            send_sem=small_send.at[kind, k], recv_sem=small_recv.at[kind, k],
            device_id=to, device_id_type=MESH,
        )

    def early_copy(k):
        return copy(early, early_in.at[k], 0, k, {"zero": peer(k)[2]})

    def peaks_copy(k):
        chip_to, core_to, to = peer(k)
        tile = pl.ds(pl.multiple_of(core_to * 8, 8), 8)
        return copy(peaks.at[chip_to, tile], peaks_in.at[k], 1, k, {"zero": to})

    own = pl.ds(pl.multiple_of(core * 8, 8), 8)

    def scales_copy(k):
        return copy(scales.at[chip, own], scales.at[chip, own], 2, k, {"zero": peer(k)[2]})

    def router_copy(k):
        return copy(router_ref.at[rank, mine], router_ref.at[rank, mine], 3, k, {"zero": peer(k)[2]})

    def cross_copy(b):
        to = lax.rem(bank + b, banks)
        return pltpu.make_async_remote_copy(
            src_ref=router_ref.at[rank], dst_ref=router_ref.at[rank],
            send_sem=cross_send.at[b - 1], recv_sem=cross_recv.at[b - 1],
            device_id={"bank": to}, device_id_type=MESH,
        )

    def block_copy(group, e0, n, k):
        to = peer(k)[2]
        return pltpu.make_async_remote_copy(
            src_ref=sent.at[to, pl.ds(e0, n)],
            dst_ref=ready_ref.at[pl.ds(e0, n), :, mine],
            send_sem=send_sem.at[group, k], recv_sem=recv_sem.at[group, k],
            device_id={"zero": to}, device_id_type=MESH,
        )

    every = range(len(PEERS))
    for k in every:
        early_copy(k).start()

    for e in range(EARLY, 8):
        load(e).wait()

    def peak_rows(block, e0):
        rows_of = [
            early[e0 + i, pl.ds(block, 1), :] if e0 + i < EARLY else peak(e0 + i, block)
            for i in range(8)
        ]
        peaks[block, pl.ds(e0, 8), :] = jnp.concatenate(rows_of, axis=0)

    pl.loop(0, chips)(lambda block: peak_rows(block, 0))
    for e in range(8, experts):
        load(e).wait()
    pl.loop(0, chips)(lambda block: peak_rows(block, 8))

    for k in every:
        peaks_copy(k).start()
    for k in every:
        router_copy(k).start()

    def scaled(e, row_of):
        for b in range(chips):
            inverse = 1.0 / row_of(b)
            column = jnp.broadcast_to(inverse, (LANES, LANES)).T
            y = (xv[e, pl.ds(b * LANES, LANES), :] * column).astype(jnp.bfloat16)
            sent[2 * b, e] = y[:per]
            sent[2 * b + 1, e] = y[per:]
        ready_ref[e, :, mine] = sent[me, e]

    for k in every:
        early_copy(k).wait_recv()
    top = early[...]
    for k in every:
        top = jnp.maximum(top, early_in[k])
    early_scale[...] = top
    for e in range(EARLY):
        scaled(e, lambda b: early_scale[e, b : b + 1, :])
        if e == 0:
            for k in every:
                block_copy(0, 0, 1, k).start()

    for k in every:
        peaks_copy(k).wait_recv()
    top = peaks[chip, own, :]
    for k in every:
        top = jnp.maximum(top, peaks_in[k])
    scales[chip, own, :] = top
    for k in every:
        scales_copy(k).start()
    for k in every:
        block_copy(1, 1, EARLY - 1, k).start()

    for k in every:
        router_copy(k).wait_recv()
    for b in range(1, banks):
        cross_copy(b).start()

    for k in every:
        scales_copy(k).wait_recv()
    whole = scales[chip]
    scale_ref[...] = jnp.where(core == 0, whole[:, :per], whole[:, per:])

    groups = (experts - EARLY) // GROUP

    @pl.loop(0, groups)
    def _(i):
        e0 = EARLY + i * GROUP
        for j in range(GROUP):
            e = e0 + j
            scaled(e, lambda b: scales[b, pl.ds(e, 1), :])
        for k in every:
            block_copy(2 + i, e0, GROUP, k).start()

    for k in every:
        early_copy(k).wait_send()
        peaks_copy(k).wait_send()
        scales_copy(k).wait_send()
        router_copy(k).wait_send()
    for b in range(1, banks):
        cross_copy(b).wait()
    for k in every:
        block_copy(0, 0, 1, k).wait()
        block_copy(1, 1, EARLY - 1, k).wait()

    @pl.loop(0, groups)
    def _(i):
        for k in every:
            block_copy(2 + i, EARLY + i * GROUP, GROUP, k).wait()


def solution(mesh):
    chips, banks = mesh.shape["zero"] // 2, mesh.shape["bank"]

    def per_device(train_down, router_weight, router_gain):
        experts, rows, lanes = train_down.shape
        per = rows // (2 * chips)
        columns = router_weight.shape[1]
        vmem = pl.BlockSpec(memory_space=pltpu.VMEM)
        groups = 2 + (experts - EARLY) // GROUP
        n = len(PEERS)
        ready, scale, router = pl.pallas_call(
            functools.partial(exchange_kernel, (chips, banks)),
            out_shape=(
                jax.ShapeDtypeStruct((experts, per, 2 * chips * lanes), jnp.bfloat16),
                jax.ShapeDtypeStruct((experts, per), jnp.float32),
                jax.ShapeDtypeStruct((columns * banks, 2 * chips * LANES), jnp.bfloat16),
            ),
            in_specs=[pl.BlockSpec(memory_space=pltpu.HBM), vmem, vmem],
            out_specs=(vmem, vmem, vmem),
            scratch_shapes=[
                pltpu.VMEM((experts, rows, lanes), jnp.float32),
                pltpu.VMEM((2 * chips, experts, per, lanes), jnp.bfloat16),
                pltpu.VMEM((EARLY, chips, LANES), jnp.float32),
                pltpu.VMEM((n, EARLY, chips, LANES), jnp.float32),
                pltpu.VMEM((EARLY, chips, LANES), jnp.float32),
                pltpu.VMEM((chips, experts, LANES), jnp.float32),
                pltpu.VMEM((n, 8, LANES), jnp.float32),
                pltpu.VMEM((chips, experts, LANES), jnp.float32),
                pltpu.SemaphoreType.DMA((experts,)),
                pltpu.SemaphoreType.DMA((groups, n)),
                pltpu.SemaphoreType.DMA((groups, n)),
                pltpu.SemaphoreType.DMA((4, n)),
                pltpu.SemaphoreType.DMA((4, n)),
                pltpu.SemaphoreType.DMA((banks - 1,)),
                pltpu.SemaphoreType.DMA((banks - 1,)),
            ],
            compiler_params=pltpu.CompilerParams(
                collective_id=0, has_side_effects=True, vmem_limit_bytes=40 * 2**20
            ),
            name="exchange",
        )(train_down, router_weight.T, router_gain.reshape(1, -1))
        return ready, scale, router.T

    return jax.shard_map(
        per_device,
        mesh=mesh,
        in_specs=(P(("unit", "bank"), None, "zero"), P(("unit", "zero"), "bank"), P(("unit", "zero"))),
        out_specs=(P(("unit", "bank"), "zero", None), P(("unit", "bank"), "zero"), P("unit", None)),
        check_vma=False,
    )
```

time: 209 us -> 122 us (0.58)
  blocking collectives: 122 us -> 0 us
  Pallas kernels: 0 us -> 113 us
  waiting for transfers between devices: 42.8 us -> 0 us
  between operations: 14.2 us -> 0.65 us
  other arithmetic: 12.8 us -> 0 us
  starting transfers between devices: 4.71 us -> 0 us
  local copies, waits for them, and re-layouts: 11.6 us -> 8.04 us
    all_gather x2 -> x0, blocking collectives: 115 us -> none  [the longest x1 105 us: per_device(): row_router = lax.all_gather(part_router, ZERO, axis=0, tiled=True)]
    pallas_call x0 -> x1, Pallas kernels: none -> 113 us  [per_device(): pl.pallas_call(functools.partial(exchange_kernel, (chips, banks)), out_sh...]
    all_gather x1 -> x0, waiting for transfers between devices: 42.8 us -> none  [gathered_total(): tiles = lax.all_gather(value, axis)]
    reduce_max x2 -> x0, other arithmetic: 7.53 us -> none  [the longest x1 6.25 us: per_device(): scale_down = gathered_total(jnp.max(jnp.abs(train_down), axis=2), ZERO)]
    all_to_all x1 -> x0, blocking collectives: 7.05 us -> none  [turned_blocks(): lax.all_to_all(tiles, axes[k], split_axis=k, concat_axis=k, tiled=True)]
    unnamed x20 -> x9, local copies, waits for them, and re-layouts: 1.24 us -> 8.04 us
    reshape x2 -> x0, local copies, waits for them, and re-layouts: 6.66 us -> none  [the longest x1 5.35 us: joined_along(): tiles.reshape(*dims[:dim], dims[dim] * dims[dim + 1], *dims[dim + 2:])]
    convert_element_type x2 -> x0, other arithmetic: 5.26 us -> none  [the longest x1 5.26 us: per_device(): (train_down / jnp.expand_dims(scale_down, 2)).astype(jnp.bfloat16)]
  transfers between devices with their start and end apart: 2 -> 0, of which waited for: 1 -> 0; matrix products, arithmetic and copies ran while one was open for 0% -> 0% of each run, Pallas kernels for 0% -> 0%
where the time goes in v1:
time: 122 us
  Pallas kernels  113 us (93%)
  local copies, waits for them, and re-layouts  8.04 us (7%)
    pallas_call x1, Pallas kernels, per_device(): pl.pallas_call(functools.partial(exchange_kernel, (chips, banks)), out_sh...  113 us
    unnamed x9, local copies, waits for them, and re-layouts  8.04 us

profile of v1, /device:TPU:1, one launch (start us, length us, event | category | flops | bytes accessed | tf_op | source)
XLA Modules:
  0.0 121.8 jit_solution(10968291309350231328)
XLA Ops:
  0.6 0.0 copy-start
  0.6 3.4 %copy-done = f32[16,1024,128]{2,1,0:T(8,128)S(1)} copy-done((f32[16,1024,128]{2,1,0:T(8,128)S(1)}, f32[16,1024,128]{2,1,0:T(8,128)}, u32[]{:S(2)}) %copy-start) | copy-done | bytes 8388632
  4.0 0.0 copy-start.1
  4.0 0.7 copy-done.1
  4.7 0.0 copy-start.2
  4.7 0.7 copy-done.2
  5.4 113.1 %exchange.1 = (bf16[16,64,2048]{2,1,0:T(8,128)(2,1)S(1)}, f32[16,64]{1,0:T(8,128)S(1)}, bf16[64,2048]{1,0:T(8,128)(2,1)S(1)}) custom-call(f32[16,1024,128]{2,1,0:T(8,128)S(1)} %copy-done, f32[16,128]{1,0:T(8,128)S(1)} %bitcast.4, f32[1,128]{1,0:T(1,128)S(1)} %bitcast.5), custom_call_target="tpu_custom_call" | custom-call | tf_op jit(solution)/shard_map/exchange/pallas_call | solution.py:209
  118.5 2.0 %copy.9 = bf16[16,64,2048]{2,1,0:T(8,128)(2,1)} copy(bf16[16,64,2048]{2,1,0:T(8,128)(2,1)S(1)} %get-tuple-element.12) | data formatting | bytes 8388608
  120.5 0.6 copy.10
  121.1 0.7 copy.11
Async XLA Ops:
  0.6 3.4 %copy-start = (f32[16,1024,128]{2,1,0:T(8,128)S(1)}, f32[16,1024,128]{2,1,0:T(8,128)}, u32[]{:S(2)}) copy-start(f32[16,1024,128]{2,1,0:T(8,128)} %x_ref.1) | copy-start | bytes 25165828
  4.0 0.7 copy-start.1
  4.7 0.7 copy-start.2

commit v2 on v1

v2 whole, which is shorter than its diff:
```python
import functools

import jax
import jax.numpy as jnp
from jax import lax
from jax.experimental import pallas as pl
from jax.experimental.pallas import tpu as pltpu
from jax.sharding import PartitionSpec as P

MESH = pl.DeviceIdType.MESH
LANES = 128
HALF = 8
EARLY = 2
GROUP = 2
STORES = 8

PEERS = [(d, c) for d in (4, 3, 5, 2, 6, 1, 7) for c in (0, 1)] + [(0, 1)]
ALIKE = [k for k, (d, c) in enumerate(PEERS) if c == 0]
PARTNER = len(PEERS) - 1
PEAKS, SCALES, ROUTER, FORWARD = 1, 2, 3, 4


def exchange_kernel(
    units,
    x_ref, w_ref, g_ref,
    ready_ref, scale_ref, router_ref,
    xv, wv, gv, sent, early, early_in, early_scale,
    peaks, pair_in, merged, peaks_in, scales, tiles,
    x_sem, send_sem, recv_sem, small_send, small_recv, cross_send, cross_recv,
):
    chips, banks = units
    experts, rows, _ = x_ref.shape
    per = ready_ref.shape[1]
    me = lax.axis_index("zero")
    chip, core = me // 2, lax.rem(me, 2)
    bank = lax.axis_index("bank")
    mine = pl.ds(pl.multiple_of(me * LANES, LANES), LANES)
    every = range(len(PEERS))

    def peer(k):
        ahead, other = PEERS[k]
        chip_to = lax.rem(chip + ahead, chips)
        core_to = lax.rem(core + other, 2)
        return chip_to, {"zero": chip_to * 2 + core_to}

    def load(e):
        return pltpu.make_async_copy(x_ref.at[e], xv.at[e], x_sem.at[e])

    for e in range(experts):
        load(e).start()
    weight_in = pltpu.make_async_copy(w_ref, wv, x_sem.at[experts])
    gain_in = pltpu.make_async_copy(g_ref, gv, x_sem.at[experts + 1])
    weight_in.start()
    gain_in.start()

    barrier = pltpu.get_barrier_semaphore()
    for k in every:
        pl.semaphore_signal(barrier, inc=1, device_id=peer(k)[1], device_id_type=MESH)
    for b in range(1, banks):
        to = lax.rem(bank + b, banks)
        pl.semaphore_signal(barrier, inc=1, device_id={"bank": to}, device_id_type=MESH)

    def peak(e, block):
        tile = jnp.abs(xv[e, pl.ds(block * LANES, LANES), :])
        return jnp.max(tile.T, axis=0, keepdims=True)

    for e in range(EARLY):
        load(e).wait()
        early[e] = jnp.concatenate([peak(e, b) for b in range(chips)], axis=0)

    def copy(src, dst, kind, k):
        return pltpu.make_async_remote_copy(
            src_ref=src, dst_ref=dst,
            send_sem=small_send.at[kind, k], recv_sem=small_recv.at[kind, k],
            device_id=peer(k)[1], device_id_type=MESH,
        )

    def early_copy(k):
        return copy(early, early_in.at[k], 0, k)

    def peaks_copy(k):
        return copy(merged.at[peer(k)[0]], peaks_in.at[k], PEAKS, k)

    pair_copy = copy(peaks.at[1 - core], pair_in, PEAKS, PARTNER)

    def scales_copy(k):
        place = scales.at[core, chip]
        return copy(place, place, SCALES, k)

    scales_pass = copy(scales.at[core], scales.at[core], SCALES, PARTNER)
    rank = pl.ds(pl.multiple_of(bank * 16, 16), 16)
    column = pl.ds(pl.multiple_of(chip * LANES, LANES), LANES)

    def router_copy(k):
        place = tiles.at[core, rank, column]
        return copy(place, place, ROUTER, k)

    def cross_copy(b):
        place = tiles.at[core, rank]
        return pltpu.make_async_remote_copy(
            src_ref=place, dst_ref=place,
            send_sem=cross_send.at[b - 1], recv_sem=cross_recv.at[b - 1],
            device_id={"bank": lax.rem(bank + b, banks)}, device_id_type=MESH,
        )

    router_pass = copy(tiles.at[core], tiles.at[core], ROUTER, PARTNER)

    def block_copy(group, e0, n, k):
        chip_to, to = peer(k)
        return pltpu.make_async_remote_copy(
            src_ref=sent.at[to["zero"], pl.ds(e0, n)],
            dst_ref=ready_ref.at[pl.ds(e0, n), :, mine],
            send_sem=send_sem.at[group, k], recv_sem=recv_sem.at[group, k],
            device_id=to, device_id_type=MESH,
        )

    pl.semaphore_wait(barrier, len(PEERS) + banks - 1)
    for k in every:
        early_copy(k).start()
    for e in range(EARLY, experts):
        load(e).wait()

    def half_peaks(half):
        @pl.loop(0, chips)
        def _(block):
            found = [peak(half * HALF + i, block) for i in range(HALF)]
            peaks[half, block] = jnp.concatenate(found, axis=0)

    half_peaks(1 - core)
    pair_copy.start()
    half_peaks(core)
    pair_copy.wait_recv()
    merged[...] = jnp.maximum(peaks[core], pair_in[...])
    for k in ALIKE:
        peaks_copy(k).start()
    weight_in.wait()
    gain_in.wait()
    tiles[core, rank, column] = (wv[...] * gv[...]).astype(jnp.bfloat16)
    for k in ALIKE:
        router_copy(k).start()

    def scaled(e, row_of):
        for b in range(chips):
            inverse = 1.0 / row_of(b)
            spread = jnp.broadcast_to(inverse, (LANES, LANES)).T
            y = (xv[e, pl.ds(b * LANES, LANES), :] * spread).astype(jnp.bfloat16)
            sent[2 * b, e] = y[:per]
            sent[2 * b + 1, e] = y[per:]
        ready_ref[e, :, mine] = sent[me, e]

    for k in every:
        early_copy(k).wait_recv()
    top = early[...]
    for k in every:
        top = jnp.maximum(top, early_in[k])
    early_scale[...] = top
    for e in range(EARLY):
        scaled(e, lambda b: early_scale[e, b : b + 1, :])
        if e == 0:
            for k in every:
                block_copy(0, 0, 1, k).start()
    for k in ALIKE:
        peaks_copy(k).wait_recv()
    top = merged[chip]
    for k in ALIKE:
        top = jnp.maximum(top, peaks_in[k])
    scales[core, chip] = top
    for k in ALIKE:
        scales_copy(k).start()
    for k in every:
        block_copy(1, 1, EARLY - 1, k).start()
    for k in ALIKE:
        router_copy(k).wait_recv()
    for b in range(1, banks):
        cross_copy(b).start()
    for k in ALIKE:
        scales_copy(k).wait_recv()
    scales_pass.start()
    scales_pass.wait_recv()
    groups = (experts - EARLY) // GROUP

    @pl.loop(0, groups)
    def _(i):
        e0 = EARLY + i * GROUP
        for j in range(GROUP):
            e = e0 + j
            scaled(e, lambda b: scales[e // HALF, b, pl.ds(lax.rem(e, HALF), 1), :])
        for k in every:
            block_copy(2 + i, e0, GROUP, k).start()

    whole = jnp.concatenate([scales[0, chip], scales[1, chip]], axis=0)
    scale_ref[...] = jnp.where(core == 0, whole[:, :per], whole[:, per:])
    for b in range(1, banks):
        cross_copy(b).wait()
    router_pass.start()
    router_pass.wait()
    for j in range(chips):
        for c in range(2):
            at = (2 * j + c) * LANES
            router_ref[:, at : at + LANES] = tiles[c, :, j * LANES : (j + 1) * LANES]
    for k in every:
        early_copy(k).wait_send()
    for k in ALIKE:
        peaks_copy(k).wait_send()
        scales_copy(k).wait_send()
        router_copy(k).wait_send()
    pair_copy.wait_send()
    scales_pass.wait_send()
    for k in every:
        block_copy(0, 0, 1, k).wait()
        block_copy(1, 1, EARLY - 1, k).wait()

    @pl.loop(0, groups)
    def _(i):
        for k in every:
            block_copy(2 + i, EARLY + i * GROUP, GROUP, k).wait()


def store_kernel(ready, scale, router, ready_ref, scale_ref, router_ref, sem):
    step = ready.shape[0] // STORES
    parts = [pl.ds(i * step, step) for i in range(STORES)]
    moves = [(ready.at[p], ready_ref.at[p]) for p in parts]
    moves += [(scale, scale_ref), (router, router_ref)]
    copies = [pltpu.make_async_copy(*m, sem.at[i]) for i, m in enumerate(moves)]
    for c in copies:
        c.start()
    for c in copies:
        c.wait()


def solution(mesh):
    chips, banks = mesh.shape["zero"] // 2, mesh.shape["bank"]

    def per_device(train_down, router_weight, router_gain):
        experts, rows, lanes = train_down.shape
        per = rows // (2 * chips)
        columns = router_weight.shape[1]
        vmem = pl.BlockSpec(memory_space=pltpu.VMEM)
        hbm = pl.BlockSpec(memory_space=pltpu.HBM)
        groups = 2 + (experts - EARLY) // GROUP
        n = len(PEERS)
        outs = (
            jax.ShapeDtypeStruct((experts, per, 2 * chips * lanes), jnp.bfloat16),
            jax.ShapeDtypeStruct((experts, per), jnp.float32),
            jax.ShapeDtypeStruct((columns * banks, 2 * chips * LANES), jnp.bfloat16),
        )
        held = [
            pltpu.with_memory_space_constraint(a, pltpu.HBM)
            for a in (train_down, router_weight.T, router_gain.reshape(1, -1))
        ]
        made = pl.pallas_call(
            functools.partial(exchange_kernel, (chips, banks)),
            out_shape=outs,
            in_specs=[hbm, hbm, hbm],
            out_specs=(vmem, vmem, vmem),
            scratch_shapes=[
                pltpu.VMEM((experts, rows, lanes), jnp.float32),
                pltpu.VMEM((columns, LANES), jnp.float32),
                pltpu.VMEM((1, LANES), jnp.float32),
                pltpu.VMEM((2 * chips, experts, per, lanes), jnp.bfloat16),
                pltpu.VMEM((EARLY, chips, LANES), jnp.float32),
                pltpu.VMEM((n, EARLY, chips, LANES), jnp.float32),
                pltpu.VMEM((EARLY, chips, LANES), jnp.float32),
                pltpu.VMEM((2, chips, HALF, LANES), jnp.float32),
                pltpu.VMEM((chips, HALF, LANES), jnp.float32),
                pltpu.VMEM((chips, HALF, LANES), jnp.float32),
                pltpu.VMEM((n, HALF, LANES), jnp.float32),
                pltpu.VMEM((2, chips, HALF, LANES), jnp.float32),
                pltpu.VMEM((2, columns * banks, chips * LANES), jnp.bfloat16),
                pltpu.SemaphoreType.DMA((experts + 2,)),
                pltpu.SemaphoreType.DMA((groups, n)),
                pltpu.SemaphoreType.DMA((groups, n)),
                pltpu.SemaphoreType.DMA((4, n)),
                pltpu.SemaphoreType.DMA((4, n)),
                pltpu.SemaphoreType.DMA((banks - 1,)),
                pltpu.SemaphoreType.DMA((banks - 1,)),
            ],
            compiler_params=pltpu.CompilerParams(
                collective_id=0, has_side_effects=True, vmem_limit_bytes=24 * 2**20
            ),
            name="exchange",
        )(*held)
        ready, scale, router = pl.pallas_call(
            store_kernel,
            out_shape=outs,
            in_specs=[vmem, vmem, vmem],
            out_specs=(hbm, hbm, hbm),
            scratch_shapes=[pltpu.SemaphoreType.DMA((STORES + 2,))],
            compiler_params=pltpu.CompilerParams(vmem_limit_bytes=4 * 2**20),
            name="store",
        )(*(pltpu.with_memory_space_constraint(a, pltpu.VMEM) for a in made))
        return ready, scale, router.T

    return jax.shard_map(
        per_device,
        mesh=mesh,
        in_specs=(P(("unit", "bank"), None, "zero"), P(("unit", "zero"), "bank"), P(("unit", "zero"))),
        out_specs=(P(("unit", "bank"), "zero", None), P(("unit", "bank"), "zero"), P("unit", None)),
        check_vma=False,
    )
```

time: 122 us -> 115 us (0.943)
  local copies, waits for them, and re-layouts: 8.04 us -> 0 us
    unnamed x9 -> x0, local copies, waits for them, and re-layouts: 8.04 us -> none
    pallas_call x0 -> x1, Pallas kernels: none -> 2.18 us  [per_device(): pl.pallas_call(store_kernel, out_shape=outs, in_specs=[vmem, vmem, vmem],...]
where the time goes in v2:
time: 115 us
  Pallas kernels  114 us (99%)
    pallas_call x1, Pallas kernels, per_device(): pl.pallas_call(functools.partial(exchange_kernel, (chips, banks)), out_sh...  112 us

profile of v2, /device:TPU:1, one launch (start us, length us, event | category | flops | bytes accessed | tf_op | source)
XLA Modules:
  0.0 114.7 jit_solution(623686427262943499)
XLA Ops:
  0.6 111.9 %exchange.1 = (bf16[16,64,2048]{2,1,0:T(8,128)(2,1)S(1)}, f32[16,64]{1,0:T(8,128)S(1)}, bf16[64,2048]{1,0:T(8,128)(2,1)S(1)}) custom-call(f32[16,1024,128]{2,1,0:T(8,128)} %x_ref.1, f32[16,128]{1,0:T(8,128)} %bitcast.3, f32[1,128]{1,0:T(1,128)} %bitcast.4), custom_call_target="tpu_custom_call" | custom-call | tf_op jit(solution)/shard_map/exchange/pallas_call | solution.py:251
  112.6 2.2 %store.1 = (bf16[16,64,2048]{2,1,0:T(8,128)(2,1)}, f32[16,64]{1,0:T(8,128)}, bf16[64,2048]{1,0:T(8,128)(2,1)}) custom-call(bf16[16,64,2048]{2,1,0:T(8,128)(2,1)S(1)} %get-tuple-element.9.ready, f32[16,64]{1,0:T(8,128)S(1)} %get-tuple-element.10.scale, bf16[64,2048]{1,0:T(8,128)(2,1)S(1)} %get-tuple-element.11.router), custom_call_target="tpu_custom_call" | custom-call | tf_op jit(solution)/shard_map/store/pallas_call | solution.py:283

commit v3 on v2

--- a/solution.py
+++ b/solution.py
@@ -17,7 +17,7 @@
 PEERS = [(d, c) for d in (4, 3, 5, 2, 6, 1, 7) for c in (0, 1)] + [(0, 1)]
 ALIKE = [k for k, (d, c) in enumerate(PEERS) if c == 0]
 PARTNER = len(PEERS) - 1
-PEAKS, SCALES, ROUTER, FORWARD = 1, 2, 3, 4
+FIRST, PEAKS, SCALES, ROUTER, PAIR, PASS, SIDE, WHOLE, BLOCKS = range(9)
 
 
 def exchange_kernel(
@@ -26,7 +26,7 @@
     ready_ref, scale_ref, router_ref,
     xv, wv, gv, sent, early, early_in, early_scale,
     peaks, pair_in, merged, peaks_in, scales, tiles,
-    x_sem, send_sem, recv_sem, small_send, small_recv, cross_send, cross_recv,
+    x_sem, send_sem, recv_sem,
 ):
     chips, banks = units
     experts, rows, _ = x_ref.shape
@@ -68,28 +68,32 @@
         load(e).wait()
         early[e] = jnp.concatenate([peak(e, b) for b in range(chips)], axis=0)
 
-    def copy(src, dst, kind, k):
+    def copy(src, dst, kind, k, to=None):
         return pltpu.make_async_remote_copy(
             src_ref=src, dst_ref=dst,
-            send_sem=small_send.at[kind, k], recv_sem=small_recv.at[kind, k],
-            device_id=peer(k)[1], device_id_type=MESH,
+            send_sem=send_sem.at[kind], recv_sem=recv_sem.at[kind],
+            device_id=peer(k)[1] if to is None else to, device_id_type=MESH,
         )
 
+    def await_all(ref, sem):
+        pltpu.make_async_copy(ref, ref, sem).wait()
+
     def early_copy(k):
-        return copy(early, early_in.at[k], 0, k)
+        return copy(early, early_in.at[k], FIRST, k)
 
     def peaks_copy(k):
-        return copy(merged.at[peer(k)[0]], peaks_in.at[k], PEAKS, k)
-
-    pair_copy = copy(peaks.at[1 - core], pair_in, PEAKS, PARTNER)
+        return copy(merged.at[peer(k)[0]], peaks_in.at[k // 2], PEAKS, k)
+
+    pair_copy = copy(peaks.at[1 - core], pair_in, PAIR, PARTNER)
 
     def scales_copy(k):
         place = scales.at[core, chip]
         return copy(place, place, SCALES, k)
 
-    scales_pass = copy(scales.at[core], scales.at[core], SCALES, PARTNER)
+    scales_pass = copy(scales.at[core], scales.at[core], PASS, PARTNER)
     rank = pl.ds(pl.multiple_of(bank * 16, 16), 16)
     column = pl.ds(pl.multiple_of(chip * LANES, LANES), LANES)
+    sevenths = tiles.at[0, pl.ds(0, 16), pl.ds(0, (chips - 1) * LANES)]
 
     def router_copy(k):
         place = tiles.at[core, rank, column]
@@ -97,22 +101,14 @@
 
     def cross_copy(b):
         place = tiles.at[core, rank]
-        return pltpu.make_async_remote_copy(
-            src_ref=place, dst_ref=place,
-            send_sem=cross_send.at[b - 1], recv_sem=cross_recv.at[b - 1],
-            device_id={"bank": lax.rem(bank + b, banks)}, device_id_type=MESH,
-        )
-
-    router_pass = copy(tiles.at[core], tiles.at[core], ROUTER, PARTNER)
-
-    def block_copy(group, e0, n, k):
-        chip_to, to = peer(k)
-        return pltpu.make_async_remote_copy(
-            src_ref=sent.at[to["zero"], pl.ds(e0, n)],
-            dst_ref=ready_ref.at[pl.ds(e0, n), :, mine],
-            send_sem=send_sem.at[group, k], recv_sem=recv_sem.at[group, k],
-            device_id=to, device_id_type=MESH,
-        )
+        return copy(place, place, SIDE, None, {"bank": lax.rem(bank + b, banks)})
+
+    router_pass = copy(tiles.at[core], tiles.at[core], WHOLE, PARTNER)
+
+    def block_copy(e0, n, k):
+        to = peer(k)[1]
+        experts_of = pl.ds(e0, n)
+        return copy(sent.at[to["zero"], experts_of], ready_ref.at[experts_of, :, mine], BLOCKS, k)
 
     pl.semaphore_wait(barrier, len(PEERS) + banks - 1)
     for k in every:
@@ -148,8 +144,7 @@
             sent[2 * b + 1, e] = y[per:]
         ready_ref[e, :, mine] = sent[me, e]
 
-    for k in every:
-        early_copy(k).wait_recv()
+    await_all(early_in, recv_sem.at[FIRST])
     top = early[...]
     for k in every:
         top = jnp.maximum(top, early_in[k])
@@ -158,23 +153,20 @@
         scaled(e, lambda b: early_scale[e, b : b + 1, :])
         if e == 0:
             for k in every:
-                block_copy(0, 0, 1, k).start()
-    for k in ALIKE:
-        peaks_copy(k).wait_recv()
+                block_copy(0, 1, k).start()
+    await_all(peaks_in, recv_sem.at[PEAKS])
     top = merged[chip]
     for k in ALIKE:
-        top = jnp.maximum(top, peaks_in[k])
+        top = jnp.maximum(top, peaks_in[k // 2])
     scales[core, chip] = top
     for k in ALIKE:
         scales_copy(k).start()
     for k in every:
-        block_copy(1, 1, EARLY - 1, k).start()
-    for k in ALIKE:
-        router_copy(k).wait_recv()
+        block_copy(1, EARLY - 1, k).start()
+    await_all(sevenths, recv_sem.at[ROUTER])
     for b in range(1, banks):
         cross_copy(b).start()
-    for k in ALIKE:
-        scales_copy(k).wait_recv()
+    await_all(peaks_in, recv_sem.at[SCALES])
     scales_pass.start()
     scales_pass.wait_recv()
     groups = (experts - EARLY) // GROUP
@@ -186,34 +178,27 @@
             e = e0 + j
             scaled(e, lambda b: scales[e // HALF, b, pl.ds(lax.rem(e, HALF), 1), :])
         for k in every:
-            block_copy(2 + i, e0, GROUP, k).start()
+            block_copy(e0, GROUP, k).start()
 
     whole = jnp.concatenate([scales[0, chip], scales[1, chip]], axis=0)
     scale_ref[...] = jnp.where(core == 0, whole[:, :per], whole[:, per:])
-    for b in range(1, banks):
-        cross_copy(b).wait()
+    await_all(tiles.at[core, pl.ds(0, 16 * (banks - 1))], recv_sem.at[SIDE])
     router_pass.start()
     router_pass.wait()
     for j in range(chips):
         for c in range(2):
             at = (2 * j + c) * LANES
             router_ref[:, at : at + LANES] = tiles[c, :, j * LANES : (j + 1) * LANES]
-    for k in every:
-        early_copy(k).wait_send()
-    for k in ALIKE:
-        peaks_copy(k).wait_send()
-        scales_copy(k).wait_send()
-        router_copy(k).wait_send()
+    await_all(early_in, send_sem.at[FIRST])
+    await_all(peaks_in, send_sem.at[PEAKS])
+    await_all(peaks_in, send_sem.at[SCALES])
+    await_all(sevenths, send_sem.at[ROUTER])
+    await_all(tiles.at[core, pl.ds(0, 16 * (banks - 1))], send_sem.at[SIDE])
     pair_copy.wait_send()
     scales_pass.wait_send()
-    for k in every:
-        block_copy(0, 0, 1, k).wait()
-        block_copy(1, 1, EARLY - 1, k).wait()
-
-    @pl.loop(0, groups)
-    def _(i):
-        for k in every:
-            block_copy(2 + i, EARLY + i * GROUP, GROUP, k).wait()
+    blocks = sent.at[pl.ds(0, len(PEERS))]
+    await_all(blocks, send_sem.at[BLOCKS])
+    await_all(blocks, recv_sem.at[BLOCKS])
 
 
 def store_kernel(ready, scale, router, ready_ref, scale_ref, router_ref, sem):
@@ -237,7 +222,6 @@
         columns = router_weight.shape[1]
         vmem = pl.BlockSpec(memory_space=pltpu.VMEM)
         hbm = pl.BlockSpec(memory_space=pltpu.HBM)
-        groups = 2 + (experts - EARLY) // GROUP
         n = len(PEERS)
         outs = (
             jax.ShapeDtypeStruct((experts, per, 2 * chips * lanes), jnp.bfloat16),
@@ -264,16 +248,12 @@
                 pltpu.VMEM((2, chips, HALF, LANES), jnp.float32),
                 pltpu.VMEM((chips, HALF, LANES), jnp.float32),
                 pltpu.VMEM((chips, HALF, LANES), jnp.float32),
-                pltpu.VMEM((n, HALF, LANES), jnp.float32),
+                pltpu.VMEM((chips - 1, HALF, LANES), jnp.float32),
                 pltpu.VMEM((2, chips, HALF, LANES), jnp.float32),
                 pltpu.VMEM((2, columns * banks, chips * LANES), jnp.bfloat16),
                 pltpu.SemaphoreType.DMA((experts + 2,)),
-                pltpu.SemaphoreType.DMA((groups, n)),
-                pltpu.SemaphoreType.DMA((groups, n)),
-                pltpu.SemaphoreType.DMA((4, n)),
-                pltpu.SemaphoreType.DMA((4, n)),
-                pltpu.SemaphoreType.DMA((banks - 1,)),
-                pltpu.SemaphoreType.DMA((banks - 1,)),
+                pltpu.SemaphoreType.DMA((BLOCKS + 1,)),
+                pltpu.SemaphoreType.DMA((BLOCKS + 1,)),
             ],
             compiler_params=pltpu.CompilerParams(
                 collective_id=0, has_side_effects=True, vmem_limit_bytes=24 * 2**20

time: 115 us -> 111 us (0.965)
  Pallas kernels: 114 us -> 110 us
    pallas_call x1, Pallas kernels: 112 us -> 108 us  [per_device(): pl.pallas_call(functools.partial(exchange_kernel, (chips, banks)), out_sh...]
where the time goes in v3:
time: 111 us
  Pallas kernels  110 us (99%)
    pallas_call x1, Pallas kernels, per_device(): pl.pallas_call(functools.partial(exchange_kernel, (chips, banks)), out_sh...  108 us

profile of v3, /device:TPU:1, one launch (start us, length us, event | category | flops | bytes accessed | tf_op | source)
XLA Modules:
  0.0 110.6 jit_solution(4684452537607810240)
XLA Ops:
  0.6 107.8 %exchange.1 = (bf16[16,64,2048]{2,1,0:T(8,128)(2,1)S(1)}, f32[16,64]{1,0:T(8,128)S(1)}, bf16[64,2048]{1,0:T(8,128)(2,1)S(1)}) custom-call(f32[16,1024,128]{2,1,0:T(8,128)} %x_ref.1, f32[16,128]{1,0:T(8,128)} %bitcast.3, f32[1,128]{1,0:T(1,128)} %bitcast.4), custom_call_target="tpu_custom_call" | custom-call | tf_op jit(solution)/shard_map/exchange/pallas_call | solution.py:235
  108.4 2.2 %store.1 = (bf16[16,64,2048]{2,1,0:T(8,128)(2,1)}, f32[16,64]{1,0:T(8,128)}, bf16[64,2048]{1,0:T(8,128)(2,1)}) custom-call(bf16[16,64,2048]{2,1,0:T(8,128)(2,1)S(1)} %get-tuple-element.9.ready, f32[16,64]{1,0:T(8,128)S(1)} %get-tuple-element.10.scale, bf16[64,2048]{1,0:T(8,128)(2,1)S(1)} %get-tuple-element.11.router), custom_call_target="tpu_custom_call" | custom-call | tf_op jit(solution)/shard_map/store/pallas_call | solution.py:263

commit v4 on v3

--- a/solution.py
+++ b/solution.py
@@ -14,7 +14,7 @@
 GROUP = 2
 STORES = 8
 
-PEERS = [(d, c) for d in (4, 3, 5, 2, 6, 1, 7) for c in (0, 1)] + [(0, 1)]
+PEERS = [(d, c) for c in (1, 0) for d in (4, 3, 5, 2, 6, 1, 7)] + [(0, 1)]
 ALIKE = [k for k, (d, c) in enumerate(PEERS) if c == 0]
 PARTNER = len(PEERS) - 1
 FIRST, PEAKS, SCALES, ROUTER, PAIR, PASS, SIDE, WHOLE, BLOCKS = range(9)
@@ -82,7 +82,7 @@
         return copy(early, early_in.at[k], FIRST, k)
 
     def peaks_copy(k):
-        return copy(merged.at[peer(k)[0]], peaks_in.at[k // 2], PEAKS, k)
+        return copy(merged.at[peer(k)[0]], peaks_in.at[ALIKE.index(k)], PEAKS, k)
 
     pair_copy = copy(peaks.at[1 - core], pair_in, PAIR, PARTNER)
 
@@ -152,15 +152,17 @@
     for e in range(EARLY):
         scaled(e, lambda b: early_scale[e, b : b + 1, :])
         if e == 0:
-            for k in every:
+            for k in every[:7]:
                 block_copy(0, 1, k).start()
     await_all(peaks_in, recv_sem.at[PEAKS])
     top = merged[chip]
     for k in ALIKE:
-        top = jnp.maximum(top, peaks_in[k // 2])
+        top = jnp.maximum(top, peaks_in[ALIKE.index(k)])
     scales[core, chip] = top
     for k in ALIKE:
         scales_copy(k).start()
+    for k in every[7:]:
+        block_copy(0, 1, k).start()
     for k in every:
         block_copy(1, EARLY - 1, k).start()
     await_all(sevenths, recv_sem.at[ROUTER])

time: 111 us -> 109 us (0.982)
    pallas_call x1, Pallas kernels: 108 us -> 106 us  [per_device(): pl.pallas_call(functools.partial(exchange_kernel, (chips, banks)), out_sh...]
where the time goes in v4:
time: 109 us
  Pallas kernels  109 us (100%)
    pallas_call x1, Pallas kernels, per_device(): pl.pallas_call(functools.partial(exchange_kernel, (chips, banks)), out_sh...  106 us

profile of v4, /device:TPU:1, one launch (start us, length us, event | category | flops | bytes accessed | tf_op | source)
XLA Modules:
  0.0 109.2 jit_solution(17360108483337532487)
XLA Ops:
  0.6 106.4 %exchange.1 = (bf16[16,64,2048]{2,1,0:T(8,128)(2,1)S(1)}, f32[16,64]{1,0:T(8,128)S(1)}, bf16[64,2048]{1,0:T(8,128)(2,1)S(1)}) custom-call(f32[16,1024,128]{2,1,0:T(8,128)} %x_ref.1, f32[16,128]{1,0:T(8,128)} %bitcast.3, f32[1,128]{1,0:T(1,128)} %bitcast.4), custom_call_target="tpu_custom_call" | custom-call | tf_op jit(solution)/shard_map/exchange/pallas_call | solution.py:237
  107.1 2.2 %store.1 = (bf16[16,64,2048]{2,1,0:T(8,128)(2,1)}, f32[16,64]{1,0:T(8,128)}, bf16[64,2048]{1,0:T(8,128)(2,1)}) custom-call(bf16[16,64,2048]{2,1,0:T(8,128)(2,1)S(1)} %get-tuple-element.9.ready, f32[16,64]{1,0:T(8,128)S(1)} %get-tuple-element.10.scale, bf16[64,2048]{1,0:T(8,128)(2,1)S(1)} %get-tuple-element.11.router), custom_call_target="tpu_custom_call" | custom-call | tf_op jit(solution)/shard_map/store/pallas_call | solution.py:265

commit v5 on v4

--- a/solution.py
+++ b/solution.py
@@ -12,6 +12,8 @@
 HALF = 8
 EARLY = 2
 GROUP = 2
+TAIL = 6
+TIERS = (0, 2, 4)
 STORES = 8
 
 PEERS = [(d, c) for c in (1, 0) for d in (4, 3, 5, 2, 6, 1, 7)] + [(0, 1)]
@@ -171,16 +173,33 @@
     await_all(peaks_in, recv_sem.at[SCALES])
     scales_pass.start()
     scales_pass.wait_recv()
-    groups = (experts - EARLY) // GROUP
-
-    @pl.loop(0, groups)
-    def _(i):
-        e0 = EARLY + i * GROUP
+    def scale_group(e0):
         for j in range(GROUP):
             e = e0 + j
             scaled(e, lambda b: scales[e // HALF, b, pl.ds(lax.rem(e, HALF), 1), :])
+
+    tail = experts - TAIL
+
+    @pl.loop(0, (tail - EARLY) // GROUP)
+    def _(i):
+        scale_group(EARLY + i * GROUP)
         for k in every:
-            block_copy(e0, GROUP, k).start()
+            block_copy(EARLY + i * GROUP, GROUP, k).start()
+
+    pl.loop(0, TAIL // GROUP)(lambda i: scale_group(tail + i * GROUP))
+
+    def tail_blocks(first, past):
+        @pl.loop(0, TAIL // GROUP)
+        def _(i):
+            for k in every:
+                to = peer(k)[0]
+
+                @pl.when((to >= first) & (to < past))
+                def _():
+                    block_copy(tail + i * GROUP, GROUP, k).start()
+
+    for first, past in zip(TIERS, TIERS[1:] + (chips,)):
+        tail_blocks(first, past)
 
     whole = jnp.concatenate([scales[0, chip], scales[1, chip]], axis=0)
     scale_ref[...] = jnp.where(core == 0, whole[:, :per], whole[:, per:])

time: 109 us -> 108 us (level)
  Pallas kernels: 109 us -> 107 us
    pallas_call x1, Pallas kernels: 106 us -> 105 us  [per_device(): pl.pallas_call(functools.partial(exchange_kernel, (chips, banks)), out_sh...]
where the time goes in v5:
time: 108 us
  Pallas kernels  107 us (99%)
    pallas_call x1, Pallas kernels, per_device(): pl.pallas_call(functools.partial(exchange_kernel, (chips, banks)), out_sh...  105 us
    pallas_call x1, Pallas kernels, per_device(): pl.pallas_call(store_kernel, out_shape=outs, in_specs=[vmem, vmem, vmem],...  2.18 us

profile of v5, /device:TPU:1, one launch (start us, length us, event | category | flops | bytes accessed | tf_op | source)
XLA Modules:
  0.0 108.0 jit_solution(10674510170287344095)
XLA Ops:
  0.6 105.2 %exchange.1 = (bf16[16,64,2048]{2,1,0:T(8,128)(2,1)S(1)}, f32[16,64]{1,0:T(8,128)S(1)}, bf16[64,2048]{1,0:T(8,128)(2,1)S(1)}) custom-call(f32[16,1024,128]{2,1,0:T(8,128)} %x_ref.1, f32[16,128]{1,0:T(8,128)} %bitcast.3, f32[1,128]{1,0:T(1,128)} %bitcast.4), custom_call_target="tpu_custom_call" | custom-call | tf_op jit(solution)/shard_map/exchange/pallas_call | solution.py:256
  105.9 2.2 %store.1 = (bf16[16,64,2048]{2,1,0:T(8,128)(2,1)}, f32[16,64]{1,0:T(8,128)}, bf16[64,2048]{1,0:T(8,128)(2,1)}) custom-call(bf16[16,64,2048]{2,1,0:T(8,128)(2,1)S(1)} %get-tuple-element.9.ready, f32[16,64]{1,0:T(8,128)S(1)} %get-tuple-element.10.scale, bf16[64,2048]{1,0:T(8,128)(2,1)S(1)} %get-tuple-element.11.router), custom_call_target="tpu_custom_call" | custom-call | tf_op jit(solution)/shard_map/store/pallas_call | solution.py:284

commit v6 on v5

--- a/solution.py
+++ b/solution.py
@@ -19,7 +19,7 @@
 PEERS = [(d, c) for c in (1, 0) for d in (4, 3, 5, 2, 6, 1, 7)] + [(0, 1)]
 ALIKE = [k for k, (d, c) in enumerate(PEERS) if c == 0]
 PARTNER = len(PEERS) - 1
-FIRST, PEAKS, SCALES, ROUTER, PAIR, PASS, SIDE, WHOLE, BLOCKS = range(9)
+FIRST, SECOND, PEAKS, SCALES, ROUTER, PAIR, PASS, SIDE, WHOLE, BLOCKS = range(10)
 
 
 def exchange_kernel(
@@ -80,8 +80,8 @@
     def await_all(ref, sem):
         pltpu.make_async_copy(ref, ref, sem).wait()
 
-    def early_copy(k):
-        return copy(early, early_in.at[k], FIRST, k)
+    def early_copy(i, k):
+        return copy(early.at[i], early_in.at[i, k], FIRST + i, k)
 
     def peaks_copy(k):
         return copy(merged.at[peer(k)[0]], peaks_in.at[ALIKE.index(k)], PEAKS, k)
@@ -113,8 +113,9 @@
         return copy(sent.at[to["zero"], experts_of], ready_ref.at[experts_of, :, mine], BLOCKS, k)
 
     pl.semaphore_wait(barrier, len(PEERS) + banks - 1)
-    for k in every:
-        early_copy(k).start()
+    for i in range(EARLY):
+        for k in every:
+            early_copy(i, k).start()
     for e in range(EARLY, experts):
         load(e).wait()
 
@@ -146,12 +147,9 @@
             sent[2 * b + 1, e] = y[per:]
         ready_ref[e, :, mine] = sent[me, e]
 
-    await_all(early_in, recv_sem.at[FIRST])
-    top = early[...]
-    for k in every:
-        top = jnp.maximum(top, early_in[k])
-    early_scale[...] = top
     for e in range(EARLY):
+        await_all(early_in.at[e], recv_sem.at[FIRST + e])
+        early_scale[e] = functools.reduce(jnp.maximum, [early_in[e, k] for k in every], early[e])
         scaled(e, lambda b: early_scale[e, b : b + 1, :])
         if e == 0:
             for k in every[:7]:
@@ -210,7 +208,8 @@
         for c in range(2):
             at = (2 * j + c) * LANES
             router_ref[:, at : at + LANES] = tiles[c, :, j * LANES : (j + 1) * LANES]
-    await_all(early_in, send_sem.at[FIRST])
+    for e in range(EARLY):
+        await_all(early_in.at[e], send_sem.at[FIRST + e])
     await_all(peaks_in, send_sem.at[PEAKS])
     await_all(peaks_in, send_sem.at[SCALES])
     await_all(sevenths, send_sem.at[ROUTER])
@@ -264,7 +263,7 @@
                 pltpu.VMEM((1, LANES), jnp.float32),
                 pltpu.VMEM((2 * chips, experts, per, lanes), jnp.bfloat16),
                 pltpu.VMEM((EARLY, chips, LANES), jnp.float32),
-                pltpu.VMEM((n, EARLY, chips, LANES), jnp.float32),
+                pltpu.VMEM((EARLY, n, chips, LANES), jnp.float32),
                 pltpu.VMEM((EARLY, chips, LANES), jnp.float32),
                 pltpu.VMEM((2, chips, HALF, LANES), jnp.float32),
                 pltpu.VMEM((chips, HALF, LANES), jnp.float32),

time: 108 us -> 108 us (level)
  the two profiles are of different devices: /device:TPU:1 before, /device:TPU:66 now
where the time goes in v6:
time: 108 us
  Pallas kernels  107 us (99%)
    pallas_call x1, Pallas kernels, per_device(): pl.pallas_call(functools.partial(exchange_kernel, (chips, banks)), out_sh...  105 us
    pallas_call x1, Pallas kernels, per_device(): pl.pallas_call(store_kernel, out_shape=outs, in_specs=[vmem, vmem, vmem],...  2.18 us

profile of v6, /device:TPU:66, one launch (start us, length us, event | category | flops | bytes accessed | tf_op | source)
XLA Modules:
  0.0 107.8 jit_solution(8828434796634823198)
XLA Ops:
  0.6 105.0 %exchange.1 = (bf16[16,64,2048]{2,1,0:T(8,128)(2,1)S(1)}, f32[16,64]{1,0:T(8,128)S(1)}, bf16[64,2048]{1,0:T(8,128)(2,1)S(1)}) custom-call(f32[16,1024,128]{2,1,0:T(8,128)} %x_ref.1, f32[16,128]{1,0:T(8,128)} %bitcast.3, f32[1,128]{1,0:T(1,128)} %bitcast.4), custom_call_target="tpu_custom_call" | custom-call | tf_op jit(solution)/shard_map/exchange/pallas_call | solution.py:255
  105.7 2.2 %store.1 = (bf16[16,64,2048]{2,1,0:T(8,128)(2,1)}, f32[16,64]{1,0:T(8,128)}, bf16[64,2048]{1,0:T(8,128)(2,1)}) custom-call(bf16[16,64,2048]{2,1,0:T(8,128)(2,1)S(1)} %get-tuple-element.9.ready, f32[16,64]{1,0:T(8,128)S(1)} %get-tuple-element.10.scale, bf16[64,2048]{1,0:T(8,128)(2,1)S(1)} %get-tuple-element.11.router), custom_call_target="tpu_custom_call" | custom-call | tf_op jit(solution)/shard_map/store/pallas_call | solution.py:283

commit v7 on v6

--- a/solution.py
+++ b/solution.py
@@ -120,10 +120,11 @@
         load(e).wait()
 
     def half_peaks(half):
-        @pl.loop(0, chips)
-        def _(block):
-            found = [peak(half * HALF + i, block) for i in range(HALF)]
-            peaks[half, block] = jnp.concatenate(found, axis=0)
+        @pl.loop(0, chips // 2)
+        def _(pair):
+            for block in (2 * pair, 2 * pair + 1):
+                found = [peak(half * HALF + i, block) for i in range(HALF)]
+                peaks[half, block] = jnp.concatenate(found, axis=0)
 
     half_peaks(1 - core)
     pair_copy.start()
@@ -147,13 +148,14 @@
             sent[2 * b + 1, e] = y[per:]
         ready_ref[e, :, mine] = sent[me, e]
 
-    for e in range(EARLY):
+    def early_scaled(e):
         await_all(early_in.at[e], recv_sem.at[FIRST + e])
         early_scale[e] = functools.reduce(jnp.maximum, [early_in[e, k] for k in every], early[e])
         scaled(e, lambda b: early_scale[e, b : b + 1, :])
-        if e == 0:
-            for k in every[:7]:
-                block_copy(0, 1, k).start()
+
+    early_scaled(0)
+    for k in every[:7]:
+        block_copy(0, 1, k).start()
     await_all(peaks_in, recv_sem.at[PEAKS])
     top = merged[chip]
     for k in ALIKE:
@@ -163,6 +165,7 @@
         scales_copy(k).start()
     for k in every[7:]:
         block_copy(0, 1, k).start()
+    early_scaled(1)
     for k in every:
         block_copy(1, EARLY - 1, k).start()
     await_all(sevenths, recv_sem.at[ROUTER])

time: 108 us -> 108 us (level)
  the two profiles are of different devices: /device:TPU:66 before, /device:TPU:86 now
where the time goes in v7:
time: 108 us
  Pallas kernels  107 us (99%)
    pallas_call x1, Pallas kernels, per_device(): pl.pallas_call(functools.partial(exchange_kernel, (chips, banks)), out_sh...  105 us
    pallas_call x1, Pallas kernels, per_device(): pl.pallas_call(store_kernel, out_shape=outs, in_specs=[vmem, vmem, vmem],...  2.18 us

profile of v7, /device:TPU:86, one launch (start us, length us, event | category | flops | bytes accessed | tf_op | source)
XLA Modules:
  0.0 107.9 jit_solution(15949188679981827360)
XLA Ops:
  0.6 105.1 %exchange.1 = (bf16[16,64,2048]{2,1,0:T(8,128)(2,1)S(1)}, f32[16,64]{1,0:T(8,128)S(1)}, bf16[64,2048]{1,0:T(8,128)(2,1)S(1)}) custom-call(f32[16,1024,128]{2,1,0:T(8,128)} %x_ref.1, f32[16,128]{1,0:T(8,128)} %bitcast.3, f32[1,128]{1,0:T(1,128)} %bitcast.4), custom_call_target="tpu_custom_call" | custom-call | tf_op jit(solution)/shard_map/exchange/pallas_call | solution.py:258
  105.7 2.2 %store.1 = (bf16[16,64,2048]{2,1,0:T(8,128)(2,1)}, f32[16,64]{1,0:T(8,128)}, bf16[64,2048]{1,0:T(8,128)(2,1)}) custom-call(bf16[16,64,2048]{2,1,0:T(8,128)(2,1)S(1)} %get-tuple-element.9.ready, f32[16,64]{1,0:T(8,128)S(1)} %get-tuple-element.10.scale, bf16[64,2048]{1,0:T(8,128)(2,1)S(1)} %get-tuple-element.11.router), custom_call_target="tpu_custom_call" | custom-call | tf_op jit(solution)/shard_map/store/pallas_call | solution.py:286

commit v8 on v7

--- a/solution.py
+++ b/solution.py
@@ -12,7 +12,7 @@
 HALF = 8
 EARLY = 2
 GROUP = 2
-TAIL = 6
+TAIL = 4
 TIERS = (0, 2, 4)
 STORES = 8
 
@@ -184,7 +184,7 @@
     @pl.loop(0, (tail - EARLY) // GROUP)
     def _(i):
         scale_group(EARLY + i * GROUP)
-        for k in every:
+        for k in [PARTNER, *every[:PARTNER]]:
             block_copy(EARLY + i * GROUP, GROUP, k).start()
 
     pl.loop(0, TAIL // GROUP)(lambda i: scale_group(tail + i * GROUP))

time: 108 us -> 108 us (level)
  the two profiles are of different devices: /device:TPU:86 before, /device:TPU:1 now
where the time goes in v8:
time: 108 us; the launch traced here: 106 us
  Pallas kernels  105 us (97%)
    pallas_call x1, Pallas kernels, per_device(): pl.pallas_call(functools.partial(exchange_kernel, (chips, banks)), out_sh...  103 us
    pallas_call x1, Pallas kernels, per_device(): pl.pallas_call(store_kernel, out_shape=outs, in_specs=[vmem, vmem, vmem],...  2.18 us

profile of v8, /device:TPU:1, one launch (start us, length us, event | category | flops | bytes accessed | tf_op | source)
XLA Modules:
  0.0 105.8 jit_solution(11698354818890190283)
XLA Ops:
  0.6 103.0 %exchange.1 = (bf16[16,64,2048]{2,1,0:T(8,128)(2,1)S(1)}, f32[16,64]{1,0:T(8,128)S(1)}, bf16[64,2048]{1,0:T(8,128)(2,1)S(1)}) custom-call(f32[16,1024,128]{2,1,0:T(8,128)} %x_ref.1, f32[16,128]{1,0:T(8,128)} %bitcast.3, f32[1,128]{1,0:T(1,128)} %bitcast.4), custom_call_target="tpu_custom_call" | custom-call | tf_op jit(solution)/shard_map/exchange/pallas_call | solution.py:258
  103.6 2.2 %store.1 = (bf16[16,64,2048]{2,1,0:T(8,128)(2,1)}, f32[16,64]{1,0:T(8,128)}, bf16[64,2048]{1,0:T(8,128)(2,1)}) custom-call(bf16[16,64,2048]{2,1,0:T(8,128)(2,1)S(1)} %get-tuple-element.9.ready, f32[16,64]{1,0:T(8,128)S(1)} %get-tuple-element.10.scale, bf16[64,2048]{1,0:T(8,128)(2,1)S(1)} %get-tuple-element.11.router), custom_call_target="tpu_custom_call" | custom-call | tf_op jit(solution)/shard_map/store/pallas_call | solution.py:286

commit v9 on v8

--- a/solution.py
+++ b/solution.py
@@ -154,7 +154,7 @@
         scaled(e, lambda b: early_scale[e, b : b + 1, :])
 
     early_scaled(0)
-    for k in every[:7]:
+    for k in every[:10]:
         block_copy(0, 1, k).start()
     await_all(peaks_in, recv_sem.at[PEAKS])
     top = merged[chip]
@@ -163,7 +163,7 @@
     scales[core, chip] = top
     for k in ALIKE:
         scales_copy(k).start()
-    for k in every[7:]:
+    for k in every[10:]:
         block_copy(0, 1, k).start()
     early_scaled(1)
     for k in every:

time: 108 us -> 109 us (level); the launches traced: 106 us -> 109 us
  Pallas kernels: 105 us -> 108 us
    pallas_call x1, Pallas kernels: 103 us -> 106 us  [per_device(): pl.pallas_call(functools.partial(exchange_kernel, (chips, banks)), out_sh...]
where the time goes in v9:
time: 109 us
  Pallas kernels  108 us (99%)
    pallas_call x1, Pallas kernels, per_device(): pl.pallas_call(functools.partial(exchange_kernel, (chips, banks)), out_sh...  106 us

profile of v9, /device:TPU:1, one launch (start us, length us, event | category | flops | bytes accessed | tf_op | source)
XLA Modules:
  0.0 108.8 jit_solution(10957219021604740014)
XLA Ops:
  0.6 106.0 %exchange.1 = (bf16[16,64,2048]{2,1,0:T(8,128)(2,1)S(1)}, f32[16,64]{1,0:T(8,128)S(1)}, bf16[64,2048]{1,0:T(8,128)(2,1)S(1)}) custom-call(f32[16,1024,128]{2,1,0:T(8,128)} %x_ref.1, f32[16,128]{1,0:T(8,128)} %bitcast.3, f32[1,128]{1,0:T(1,128)} %bitcast.4), custom_call_target="tpu_custom_call" | custom-call | tf_op jit(solution)/shard_map/exchange/pallas_call | solution.py:258
  106.6 2.2 %store.1 = (bf16[16,64,2048]{2,1,0:T(8,128)(2,1)}, f32[16,64]{1,0:T(8,128)}, bf16[64,2048]{1,0:T(8,128)(2,1)}) custom-call(bf16[16,64,2048]{2,1,0:T(8,128)(2,1)S(1)} %get-tuple-element.9.ready, f32[16,64]{1,0:T(8,128)S(1)} %get-tuple-element.10.scale, bf16[64,2048]{1,0:T(8,128)(2,1)S(1)} %get-tuple-element.11.router), custom_call_target="tpu_custom_call" | custom-call | tf_op jit(solution)/shard_map/store/pallas_call | solution.py:286
